TPU v7x, 32 devices: a whole 2x2x4 slice. The times are simulated.
32 devices in a mesh: row: 4 (over x, core), col: 8 (over z, y).
Axes of the slice: x: 2, y: 2, z: 4, core: 2. Of those that a mesh axis runs over, the one named last changes fastest.
Arguments:
- tiles: int32 [4, 8, 8, 128, 128], P('row', 'col'), may hold values from 0 to 1073741823, as said below
- slots: int32 [4, 8, 8], P('row', 'col'), may hold values from 0 to 31, as said below
- factor: float32 [4096, 256], P(('row', 'col')), may hold values from -0.5 to 0.5
- dual: float32 [4096, 256], P(('row', 'col')), may hold values from -0.5 to 0.5
Outputs:
- final_factor: float32 [4096, 256], P(('row', 'col'))
- final_dual: float32 [4096, 256], P(('row', 'col'))
- objective: float32 [3], replicated
- residual: float32 [3], replicated
Inputs may be any that keep to these rules, and one draw needn't show every extreme that they name: `slots`: for every device, 8 distinct block numbers in ascending order. The stored blocks of all devices form a symmetric pattern: the block of rows piece p and columns piece q is stored if and only if the block of rows piece q and columns piece p is; every diagonal block is stored. `tiles`: the stored block of rows piece p and columns piece q is the transpose of the one of rows piece q and columns piece p; diagonal blocks are symmetric.
All inputs are finite; a program needn't handle non-finite values.
Results may differ from a plain program's by a relative error of at most 0.005.
Values may be sent and summed in bfloat16 or wider, within the bound.
A program may use at most 64 MiB of HBM per device.

v0:
```python
import math
import jax
import jax.numpy as jnp
from jax import lax
from jax.sharding import PartitionSpec as P

ITERS = 3
penalty = 2.0
step_size = 0.25
ridge_shift = 0.1
offset = 536870912


def block_weights(integers, vertices):
    unit_scale = math.sqrt(6.0 / vertices) / 2.0**29
    return ((integers - offset).astype(jnp.float32) * unit_scale).astype(jnp.bfloat16)


def unit_rows(values):
    return values * lax.rsqrt(jnp.sum(values * values, axis=1, keepdims=True) + 1e-06)


def local(tiles, slots, factor, dual):
    row_count = lax.axis_size("row")
    col_count = lax.axis_size("col")
    piece_rows = factor.shape[0]
    columns = factor.shape[1]
    vertices = piece_rows * row_count * col_count
    weights = block_weights(tiles.reshape(tiles.shape[2], piece_rows, piece_rows), vertices)
    stored = slots.reshape(-1)
    block_row = stored // row_count
    block_col = stored % row_count

    def combine(partial_value):
        return lax.psum_scatter(partial_value, "col", scatter_dimension=0, tiled=True)

    selector = (block_row[None, :] == jnp.arange(col_count, dtype=jnp.int32)[:, None]).astype(
        jnp.float32
    )
    block_sums = jnp.sum(weights, axis=2, dtype=jnp.float32)
    edge_sums = jnp.dot(selector, block_sums, precision=lax.Precision.HIGHEST)
    degree = combine(edge_sums.reshape(-1))
    current = factor
    lagrange = dual
    projected = unit_rows(current + lagrange / penalty)
    tallies = []
    for iteration in range(ITERS):
        packed = current.astype(jnp.bfloat16)
        own_gram = lax.dot_general(
            packed, packed, (((0,), (0,)), ((), ())), preferred_element_type=jnp.float32
        )
        gram_total = lax.psum(own_gram, ("row", "col"))
        gathered = lax.all_gather(packed, "row", axis=0, tiled=True).reshape(
            -1, piece_rows, columns
        )
        chosen = gathered[block_col]
        products = jnp.einsum("tij,tjk->tik", weights, chosen, preferred_element_type=jnp.float32)
        partial_value = jnp.einsum(
            "at,tik->aik", selector, products, precision=lax.Precision.HIGHEST
        )
        coupled = combine(partial_value.reshape(col_count * piece_rows, columns))
        widened = packed.astype(jnp.float32)
        gradient = degree[:, None] * widened - coupled
        precond = columns / vertices * gram_total + ridge_shift * jnp.eye(
            columns, dtype=jnp.float32
        )
        triangle = jnp.linalg.cholesky(precond)
        descent = 2.0 * gradient - lagrange - penalty * (current - projected)
        current = current + step_size * jax.scipy.linalg.cho_solve((triangle, True), descent.T).T
        projected = unit_rows(current + lagrange / penalty)
        lagrange = lagrange + penalty * (current - projected)
        mismatch = current - projected
        local_sums = jnp.stack([jnp.sum(widened * gradient), jnp.sum(mismatch * mismatch)])
        tallies.append(local_sums)
    stacked = jnp.stack(tallies)
    stacked = lax.psum(stacked, ("row", "col"))
    objective = stacked[:, 0] / (4.0 * vertices)
    residual = stacked[:, 1] / vertices
    return (current, lagrange, objective, residual)


def solution(mesh):
    in_specs = (
        P("row", "col", None, None, None),
        P("row", "col", None),
        P(("row", "col"), None),
        P(("row", "col"), None),
    )
    out_specs = (P(("row", "col"), None), P(("row", "col"), None), P(), P())
    return jax.shard_map(local, mesh=mesh, in_specs=in_specs, out_specs=out_specs, check_vma=False)
```

profile of v0, /device:TPU:0, one launch (start us, length us, event | category | flops | bytes accessed | tf_op | source)
XLA Modules:
  0.0 669.2 jit_solution(12461409791366380685)
XLA Ops:
  10.2 7.2 %all_gather.9 = bf16[512,256]{0,1:T(8,128)(2,1)S(1)} all-gather(bf16[128,256]{0,1:T(8,128)(2,1)S(1)} %get-tuple-element.92), channel_id=1, replica_groups=mesh['row'=4,'col'=8] {'row'}, dimensions={0}, use_global_device_ids=true | all-gather | bytes 327680 | tf_op jit(solution)/shard_map/all_gather | solution.py:53
  21.8 22.3 %all-reduce.1 = f32[1024]{0:T(1024)S(1)} all-reduce(f32[1024]{0:T(1024)S(1)} %convolution_bitcast_fusion), channel_id=2, replica_groups=mesh['row'=4,'col'=8] {'col'}, use_global_device_ids=true, to_apply=%region_6.8.clone | all-reduce | flops 1024 | bytes 8192
  46.1 99.0 %all-reduce.6.cloned.1.call-done = f32[256,256]{0,1:T(8,128)} async-done(((f32[256,256]{0,1:T(8,128)}), f32[256,256]{0,1:T(8,128)}) %all-reduce.6.cloned.1.call-update) | async-done | bytes 262160 | tf_op jit(solution)/shard_map/psum | solution.py:52
  147.1 11.7 %cholesky.172 = f32[128,128]{1,0:T(8,128)S(1)} custom-call(f32[128,128]{1,0:T(8,128)S(1)} %cholesky.270), custom_call_target="Cholesky" | custom-call | tf_op jit(solution)/shard_map/jit(cholesky)/cholesky | solution.py:67
  158.9 9.8 %custom-call.17 = f32[1,128,128]{1,2,0:T(8,128)S(1)} custom-call(f32[1,128,128]{2,1,0:T(8,128)S(1)} %get-tuple-element.104), custom_call_target="InvertDiagBlocksLowerTriangular" | custom-call | tf_op jit(solution)/shard_map/jit(cholesky)/cholesky | solution.py:67
  169.2 11.7 %cholesky.189 = f32[128,128]{1,0:T(8,128)S(1)} custom-call(f32[128,128]{1,0:T(8,128)S(1)} %convolution_subtract_fusion.8), custom_call_target="Cholesky" | custom-call | tf_op jit(solution)/shard_map/jit(cholesky)/cholesky | solution.py:67
  183.0 4.2 while.6
  187.2 19.7 %custom-call.18 = f32[2,128,128]{1,2,0:T(8,128)S(1)} custom-call(f32[2,128,128]{2,1,0:T(8,128)S(1)} %get-tuple-element.26), custom_call_target="InvertDiagBlocksLowerTriangular" | custom-call | tf_op jit(solution)/shard_map/jit(_cho_solve)/triangular_solve | solution.py:69
  209.4 5.8 all_gather.10
  220.1 126.6 %all-reduce.8.cloned.1.call-done = f32[256,256]{0,1:T(8,128)} async-done(((f32[256,256]{0,1:T(8,128)}), f32[256,256]{0,1:T(8,128)}) %all-reduce.8.cloned.1.call-update) | async-done | bytes 262160 | tf_op jit(solution)/shard_map/psum | solution.py:52
  348.7 11.7 %cholesky.206 = f32[128,128]{1,0:T(8,128)S(1)} custom-call(f32[128,128]{1,0:T(8,128)S(1)} %cholesky.273), custom_call_target="Cholesky" | custom-call | tf_op jit(solution)/shard_map/jit(cholesky)/cholesky | solution.py:67
  360.4 9.8 %custom-call.19 = f32[1,128,128]{1,2,0:T(8,128)S(1)} custom-call(f32[1,128,128]{2,1,0:T(8,128)S(1)} %get-tuple-element.100), custom_call_target="InvertDiagBlocksLowerTriangular" | custom-call | tf_op jit(solution)/shard_map/jit(cholesky)/cholesky | solution.py:67
  370.7 11.7 %cholesky.223 = f32[128,128]{1,0:T(8,128)S(1)} custom-call(f32[128,128]{1,0:T(8,128)S(1)} %convolution_subtract_fusion.5), custom_call_target="Cholesky" | custom-call | tf_op jit(solution)/shard_map/jit(cholesky)/cholesky | solution.py:67
  385.1 4.2 while.7
  389.3 19.7 %custom-call.20 = f32[2,128,128]{1,2,0:T(8,128)S(1)} custom-call(f32[2,128,128]{2,1,0:T(8,128)S(1)} %get-tuple-element.27), custom_call_target="InvertDiagBlocksLowerTriangular" | custom-call | tf_op jit(solution)/shard_map/jit(_cho_solve)/triangular_solve | solution.py:69
  413.1 5.8 all_gather.11
  422.7 126.8 %all-reduce.10.cloned.1.call-done = f32[256,256]{0,1:T(8,128)} async-done(((f32[256,256]{0,1:T(8,128)}), f32[256,256]{0,1:T(8,128)}) %all-reduce.10.cloned.1.call-update) | async-done | bytes 262160 | tf_op jit(solution)/shard_map/psum | solution.py:52
  551.5 11.7 %cholesky.240 = f32[128,128]{1,0:T(8,128)S(1)} custom-call(f32[128,128]{1,0:T(8,128)S(1)} %cholesky.276), custom_call_target="Cholesky" | custom-call | tf_op jit(solution)/shard_map/jit(cholesky)/cholesky | solution.py:67
  563.3 9.8 %custom-call.21 = f32[1,128,128]{1,2,0:T(8,128)S(1)} custom-call(f32[1,128,128]{2,1,0:T(8,128)S(1)} %get-tuple-element.96), custom_call_target="InvertDiagBlocksLowerTriangular" | custom-call | tf_op jit(solution)/shard_map/jit(cholesky)/cholesky | solution.py:67
  573.6 11.7 %cholesky.257 = f32[128,128]{1,0:T(8,128)S(1)} custom-call(f32[128,128]{1,0:T(8,128)S(1)} %convolution_subtract_fusion.2), custom_call_target="Cholesky" | custom-call | tf_op jit(solution)/shard_map/jit(cholesky)/cholesky | solution.py:67
  588.0 4.3 while.8
  592.3 19.7 %custom-call.22 = f32[2,128,128]{1,2,0:T(8,128)S(1)} custom-call(f32[2,128,128]{2,1,0:T(8,128)S(1)} %get-tuple-element.28), custom_call_target="InvertDiagBlocksLowerTriangular" | custom-call | tf_op jit(solution)/shard_map/jit(_cho_solve)/triangular_solve | solution.py:69
  612.0 1.7 fusion.7
  621.5 39.2 %psum.31 = f32[3,2]{1,0:T(4,128)S(1)} all-reduce(f32[3,2]{1,0:T(4,128)S(1)} %pad_maximum_fusion), channel_id=1, replica_groups=mesh['row'=4,'col'=8] {'row','col'}, use_global_device_ids=true, to_apply=%region_22.25 | all-reduce | flops 6 | bytes 48 | tf_op jit(solution)/shard_map/psum | solution.py:76
  (159 shorter events, 54.2 us)
Async XLA Ops:
  8.0 1.1 copy-start.6
  8.0 137.1 %all-reduce.6.cloned.1.call-start = ((), (), s32[]{:S(2)}) async-start(), calls=%async_computation.3 | async-start | bytes 524288 | tf_op jit(solution)/shard_map/psum | solution.py:52
  9.2 8.3 %copy-start.4 = (s32[1,1,8,128,128]{4,3,2,1,0:T(8,128)S(1)}, s32[1,1,8,128,128]{4,3,2,1,0:T(8,128)}, u32[]{:S(2)}) copy-start(s32[1,1,8,128,128]{4,3,2,1,0:T(8,128)} %param.7) | copy-start | bytes 1572868
  10.2 7.3 %copy-start.7 = (s32[1,1,8]{2,1,0:T(1,128)S(1)}, s32[1,1,8]{2,1,0:T(1,128)}, u32[]{:S(2)}) copy-start(s32[1,1,8]{2,1,0:T(1,128)} %param.8) | copy-start | bytes 100
  10.2 196.7 %reduce-scatter.4.cloned.1.call-start = ((), (), s32[]{:S(2)}) async-start(), calls=%async_computation.4 | async-start | bytes 1179648 | tf_op jit(solution)/shard_map/reduce_scatter | solution.py:35
  21.6 325.0 %all-reduce.8.cloned.1.call-start = ((), (), s32[]{:S(2)}) async-start(), calls=%async_computation.5 | async-start | bytes 524288 | tf_op jit(solution)/shard_map/psum | solution.py:52
  44.1 0.7 copy-start.8
  146.1 1.0 copy-start
  219.4 189.6 %reduce-scatter.6.cloned.1.call-start = ((), (), s32[]{:S(2)}) async-start(), calls=%async_computation.6 | async-start | bytes 1179648 | tf_op jit(solution)/shard_map/reduce_scatter | solution.py:35
  220.0 329.5 %all-reduce.10.cloned.1.call-start = ((), (), s32[]{:S(2)}) async-start(), calls=%async_computation.7 | async-start | bytes 524288 | tf_op jit(solution)/shard_map/psum | solution.py:52
  347.6 1.0 copy-start.1
  422.2 189.8 %reduce-scatter.8.cloned.1.call-start = ((), (), s32[]{:S(2)}) async-start(), calls=%async_computation.8 | async-start | bytes 1179648 | tf_op jit(solution)/shard_map/reduce_scatter | solution.py:35
  550.5 1.0 copy-start.2
  587.9 24.1 %copy-start.5 = (f32[128,256]{0,1:T(8,128)S(1)}, f32[128,256]{0,1:T(8,128)}, u32[]{:S(2)}) copy-start(f32[128,256]{0,1:T(8,128)} %reduce-scatter.4.cloned.1.call-done) | copy-start | bytes 393220
  588.0 24.0 %copy-start.3 = (f32[128,256]{0,1:T(8,128)S(1)}, f32[128,256]{0,1:T(8,128)}, u32[]{:S(2)}) copy-start(f32[128,256]{0,1:T(8,128)} %reduce-scatter.6.cloned.1.call-done) | copy-start | bytes 393220
Sparse Core Ops, SparseCore 0:
  14.3 130.7 all-reduce.5
  219.5 127.0 all-reduce.7
  422.3 127.1 all-reduce.9
Sparse Core Ops, SparseCore 1:
  21.7 66.1 reduce-scatter.3
  223.3 63.7 reduce-scatter.5
  426.0 63.8 reduce-scatter.7
where the time goes:
time: 673 us; the launch traced here: 669 us
  waiting for transfers between devices  354 us (53%)
  other arithmetic  176 us (26%)
  blocking collectives  80.4 us (12%)
  local copies, waits for them, and re-layouts  25.8 us (4%)
  between operations  21.1 us (3%)
  matrix products  11.9 us (2%)
    psum x3, waiting for transfers between devices, local(): gram_total = lax.psum(own_gram, ('row', 'col'))  352 us
    another operation x20, other arithmetic, local(): triangle = jnp.linalg.cholesky(precond)  103 us
    another operation x7, other arithmetic, local(): jax.scipy.linalg.cho_solve((triangle, True), descent.T)  59.1 us
    psum x1, blocking collectives, local(): stacked = lax.psum(stacked, ('row', 'col'))  39.2 us
    unnamed x1, blocking collectives  22.3 us
    all_gather x3, blocking collectives, local(): lax.all_gather(packed, 'row', axis=0, tiled=True)  18.8 us
  transfers between devices with their start and end apart: 6, of which 3 were waited for; matrix products, arithmetic and copies ran while one was open for 27% of the time, Pallas kernels for 0%

commit v1 on v0

--- a/solution.py
+++ b/solution.py
@@ -73,7 +73,7 @@
         local_sums = jnp.stack([jnp.sum(widened * gradient), jnp.sum(mismatch * mismatch)])
         tallies.append(local_sums)
     stacked = jnp.stack(tallies)
-    stacked = lax.psum(stacked, ("row", "col"))
+    stacked = lax.psum(lax.psum(stacked, "col"), "row")
     objective = stacked[:, 0] / (4.0 * vertices)
     residual = stacked[:, 1] / vertices
     return (current, lagrange, objective, residual)

time: 673 us -> 660 us (0.981)
  blocking collectives: 80.4 us -> 67.4 us
    psum x1 -> x2, blocking collectives: 39.2 us -> 26.3 us  [local(): stacked = lax.psum(lax.psum(stacked, 'col'), 'row')]
  transfers between devices with their start and end apart: 6 -> 6, of which waited for: 3 -> 3; matrix products, arithmetic and copies ran while one was open for 27% -> 28% of each run, Pallas kernels for 0% -> 0%
where the time goes in v1:
time: 660 us; the launch traced here: 656 us
  waiting for transfers between devices  354 us (54%)
  other arithmetic  175 us (27%)
  blocking collectives  67.4 us (10%)
  local copies, waits for them, and re-layouts  25.8 us (4%)
  between operations  21.1 us (3%)
  matrix products  11.9 us (2%)
    psum x3, waiting for transfers between devices, local(): gram_total = lax.psum(own_gram, ('row', 'col'))  352 us
    another operation x20, other arithmetic, local(): triangle = jnp.linalg.cholesky(precond)  103 us
    another operation x7, other arithmetic, local(): jax.scipy.linalg.cho_solve((triangle, True), descent.T)  59.1 us
    psum x2, blocking collectives, local(): stacked = lax.psum(lax.psum(stacked, 'col'), 'row')  26.3 us
    unnamed x1, blocking collectives  22.3 us
    all_gather x3, blocking collectives, local(): lax.all_gather(packed, 'row', axis=0, tiled=True)  18.8 us
  transfers between devices with their start and end apart: 6, of which 3 were waited for; matrix products, arithmetic and copies ran while one was open for 28% of the time, Pallas kernels for 0%

profile of v1, /device:TPU:0, one launch (start us, length us, event | category | flops | bytes accessed | tf_op | source)
XLA Modules:
  0.0 656.3 jit_solution(9209980788818514585)
XLA Ops:
  10.2 7.2 %all_gather.9 = bf16[512,256]{0,1:T(8,128)(2,1)S(1)} all-gather(bf16[128,256]{0,1:T(8,128)(2,1)S(1)} %get-tuple-element.92), channel_id=1, replica_groups=mesh['row'=4,'col'=8] {'row'}, dimensions={0}, use_global_device_ids=true | all-gather | bytes 327680 | tf_op jit(solution)/shard_map/all_gather | solution.py:53
  21.8 22.3 %all-reduce.1 = f32[1024]{0:T(1024)S(1)} all-reduce(f32[1024]{0:T(1024)S(1)} %convolution_bitcast_fusion), channel_id=2, replica_groups=mesh['row'=4,'col'=8] {'col'}, use_global_device_ids=true, to_apply=%region_6.8.clone | all-reduce | flops 1024 | bytes 8192
  46.1 99.0 %all-reduce.6.cloned.1.call-done = f32[256,256]{0,1:T(8,128)} async-done(((f32[256,256]{0,1:T(8,128)}), f32[256,256]{0,1:T(8,128)}) %all-reduce.6.cloned.1.call-update) | async-done | bytes 262160 | tf_op jit(solution)/shard_map/psum | solution.py:52
  147.1 11.7 %cholesky.172 = f32[128,128]{1,0:T(8,128)S(1)} custom-call(f32[128,128]{1,0:T(8,128)S(1)} %cholesky.270), custom_call_target="Cholesky" | custom-call | tf_op jit(solution)/shard_map/jit(cholesky)/cholesky | solution.py:67
  158.9 9.8 %custom-call.17 = f32[1,128,128]{1,2,0:T(8,128)S(1)} custom-call(f32[1,128,128]{2,1,0:T(8,128)S(1)} %get-tuple-element.104), custom_call_target="InvertDiagBlocksLowerTriangular" | custom-call | tf_op jit(solution)/shard_map/jit(cholesky)/cholesky | solution.py:67
  169.2 11.7 %cholesky.189 = f32[128,128]{1,0:T(8,128)S(1)} custom-call(f32[128,128]{1,0:T(8,128)S(1)} %convolution_subtract_fusion.8), custom_call_target="Cholesky" | custom-call | tf_op jit(solution)/shard_map/jit(cholesky)/cholesky | solution.py:67
  183.0 4.2 while.6
  187.2 19.7 %custom-call.18 = f32[2,128,128]{1,2,0:T(8,128)S(1)} custom-call(f32[2,128,128]{2,1,0:T(8,128)S(1)} %get-tuple-element.26), custom_call_target="InvertDiagBlocksLowerTriangular" | custom-call | tf_op jit(solution)/shard_map/jit(_cho_solve)/triangular_solve | solution.py:69
  209.4 5.8 all_gather.10
  220.1 126.6 %all-reduce.8.cloned.1.call-done = f32[256,256]{0,1:T(8,128)} async-done(((f32[256,256]{0,1:T(8,128)}), f32[256,256]{0,1:T(8,128)}) %all-reduce.8.cloned.1.call-update) | async-done | bytes 262160 | tf_op jit(solution)/shard_map/psum | solution.py:52
  348.7 11.7 %cholesky.206 = f32[128,128]{1,0:T(8,128)S(1)} custom-call(f32[128,128]{1,0:T(8,128)S(1)} %cholesky.273), custom_call_target="Cholesky" | custom-call | tf_op jit(solution)/shard_map/jit(cholesky)/cholesky | solution.py:67
  360.4 9.8 %custom-call.19 = f32[1,128,128]{1,2,0:T(8,128)S(1)} custom-call(f32[1,128,128]{2,1,0:T(8,128)S(1)} %get-tuple-element.100), custom_call_target="InvertDiagBlocksLowerTriangular" | custom-call | tf_op jit(solution)/shard_map/jit(cholesky)/cholesky | solution.py:67
  370.7 11.7 %cholesky.223 = f32[128,128]{1,0:T(8,128)S(1)} custom-call(f32[128,128]{1,0:T(8,128)S(1)} %convolution_subtract_fusion.5), custom_call_target="Cholesky" | custom-call | tf_op jit(solution)/shard_map/jit(cholesky)/cholesky | solution.py:67
  385.1 4.2 while.7
  389.3 19.7 %custom-call.20 = f32[2,128,128]{1,2,0:T(8,128)S(1)} custom-call(f32[2,128,128]{2,1,0:T(8,128)S(1)} %get-tuple-element.27), custom_call_target="InvertDiagBlocksLowerTriangular" | custom-call | tf_op jit(solution)/shard_map/jit(_cho_solve)/triangular_solve | solution.py:69
  413.1 5.8 all_gather.11
  422.7 126.8 %all-reduce.10.cloned.1.call-done = f32[256,256]{0,1:T(8,128)} async-done(((f32[256,256]{0,1:T(8,128)}), f32[256,256]{0,1:T(8,128)}) %all-reduce.10.cloned.1.call-update) | async-done | bytes 262160 | tf_op jit(solution)/shard_map/psum | solution.py:52
  551.5 11.7 %cholesky.240 = f32[128,128]{1,0:T(8,128)S(1)} custom-call(f32[128,128]{1,0:T(8,128)S(1)} %cholesky.276), custom_call_target="Cholesky" | custom-call | tf_op jit(solution)/shard_map/jit(cholesky)/cholesky | solution.py:67
  563.3 9.8 %custom-call.21 = f32[1,128,128]{1,2,0:T(8,128)S(1)} custom-call(f32[1,128,128]{2,1,0:T(8,128)S(1)} %get-tuple-element.96), custom_call_target="InvertDiagBlocksLowerTriangular" | custom-call | tf_op jit(solution)/shard_map/jit(cholesky)/cholesky | solution.py:67
  573.6 11.7 %cholesky.257 = f32[128,128]{1,0:T(8,128)S(1)} custom-call(f32[128,128]{1,0:T(8,128)S(1)} %convolution_subtract_fusion.2), custom_call_target="Cholesky" | custom-call | tf_op jit(solution)/shard_map/jit(cholesky)/cholesky | solution.py:67
  588.0 4.3 while.8
  592.3 19.7 %custom-call.22 = f32[2,128,128]{1,2,0:T(8,128)S(1)} custom-call(f32[2,128,128]{2,1,0:T(8,128)S(1)} %get-tuple-element.28), custom_call_target="InvertDiagBlocksLowerTriangular" | custom-call | tf_op jit(solution)/shard_map/jit(_cho_solve)/triangular_solve | solution.py:69
  620.7 20.4 %psum.38 = f32[3,2]{1,0:T(4,128)S(1)} all-reduce(f32[3,2]{1,0:T(4,128)S(1)} %pad_maximum_fusion), channel_id=1, replica_groups=mesh['row'=4,'col'=8] {'col'}, use_global_device_ids=true, to_apply=%region_22.25 | all-reduce | flops 6 | bytes 48 | tf_op jit(solution)/shard_map/psum | solution.py:76
  641.9 5.9 psum.39
  (160 shorter events, 55.8 us)
Async XLA Ops:
  8.0 1.1 copy-start.6
  8.0 137.1 %all-reduce.6.cloned.1.call-start = ((), (), s32[]{:S(2)}) async-start(), calls=%async_computation.3 | async-start | bytes 524288 | tf_op jit(solution)/shard_map/psum | solution.py:52
  9.2 8.3 %copy-start.4 = (s32[1,1,8,128,128]{4,3,2,1,0:T(8,128)S(1)}, s32[1,1,8,128,128]{4,3,2,1,0:T(8,128)}, u32[]{:S(2)}) copy-start(s32[1,1,8,128,128]{4,3,2,1,0:T(8,128)} %param.7) | copy-start | bytes 1572868
  10.2 7.3 %copy-start.7 = (s32[1,1,8]{2,1,0:T(1,128)S(1)}, s32[1,1,8]{2,1,0:T(1,128)}, u32[]{:S(2)}) copy-start(s32[1,1,8]{2,1,0:T(1,128)} %param.8) | copy-start | bytes 100
  10.2 196.7 %reduce-scatter.4.cloned.1.call-start = ((), (), s32[]{:S(2)}) async-start(), calls=%async_computation.4 | async-start | bytes 1179648 | tf_op jit(solution)/shard_map/reduce_scatter | solution.py:35
  21.6 325.0 %all-reduce.8.cloned.1.call-start = ((), (), s32[]{:S(2)}) async-start(), calls=%async_computation.5 | async-start | bytes 524288 | tf_op jit(solution)/shard_map/psum | solution.py:52
  44.1 0.7 copy-start.8
  146.1 1.0 copy-start
  219.4 189.6 %reduce-scatter.6.cloned.1.call-start = ((), (), s32[]{:S(2)}) async-start(), calls=%async_computation.6 | async-start | bytes 1179648 | tf_op jit(solution)/shard_map/reduce_scatter | solution.py:35
  220.0 329.5 %all-reduce.10.cloned.1.call-start = ((), (), s32[]{:S(2)}) async-start(), calls=%async_computation.7 | async-start | bytes 524288 | tf_op jit(solution)/shard_map/psum | solution.py:52
  347.6 1.0 copy-start.1
  422.2 189.8 %reduce-scatter.8.cloned.1.call-start = ((), (), s32[]{:S(2)}) async-start(), calls=%async_computation.8 | async-start | bytes 1179648 | tf_op jit(solution)/shard_map/reduce_scatter | solution.py:35
  550.5 1.0 copy-start.2
  587.9 24.1 %copy-start.5 = (f32[128,256]{0,1:T(8,128)S(1)}, f32[128,256]{0,1:T(8,128)}, u32[]{:S(2)}) copy-start(f32[128,256]{0,1:T(8,128)} %reduce-scatter.4.cloned.1.call-done) | copy-start | bytes 393220
  588.0 24.0 %copy-start.3 = (f32[128,256]{0,1:T(8,128)S(1)}, f32[128,256]{0,1:T(8,128)}, u32[]{:S(2)}) copy-start(f32[128,256]{0,1:T(8,128)} %reduce-scatter.6.cloned.1.call-done) | copy-start | bytes 393220
Sparse Core Ops, SparseCore 0:
  14.3 130.7 all-reduce.5
  219.5 127.0 all-reduce.7
  422.3 127.1 all-reduce.9
Sparse Core Ops, SparseCore 1:
  21.7 66.1 reduce-scatter.3
  223.3 63.7 reduce-scatter.5
  426.0 63.8 reduce-scatter.7
